TPU v7x, 256 devices: a whole 4x4x8 slice. The times are simulated.
256 devices in a mesh: group: 4 (over x), seq: 8 (over z_hi, y), expert: 8 (over z_lo, core).
Axes of the slice: x: 4, y: 4, z: 8 (z_hi: 2, z_lo: 4; z = z_hi * 4 + z_lo), core: 2. Of those that a mesh axis runs over, the one named last changes fastest.
Arguments:
- queries: bfloat16 [32, 32, 128], P('expert', 'group')
- keys: bfloat16 [32, 1024, 8, 128], P('expert', 'seq', 'group')
- values: bfloat16 [32, 1024, 8, 128], P('expert', 'seq', 'group'), may hold values from -48 to 48
- block_of_slot: int32 [32, 64], P('expert', 'seq'), may hold values from 0 to 63, each once within a row
- lengths: int32 [32], P('expert'), may hold values from 512 to 1024
- out_proj: bfloat16 [4096, 4096], P('group', 'seq'), may hold values from -0.09375 to 0.09375
- residual: bfloat16 [32, 4096], P('expert', 'seq'), may hold values from -6 to 6
- norm_gain: bfloat16 [4096], replicated, may hold values from 0.25 to 1.75
- router: bfloat16 [4096, 8], replicated, may hold values from -0.09375 to 0.09375
- routes: int32 [32, 2], P('expert'), may hold values from 0 to 7, all different within a row; in each aligned block of 4 rows (0 to 3, 4 to 7, ...) at most 2 rows name the same one
- w_gate: bfloat16 [8, 4096, 14336], P('expert', None, ('group', 'seq')), may hold values from -0.09375 to 0.09375
- w_up: bfloat16 [8, 4096, 14336], P('expert', None, ('group', 'seq')), may hold values from -0.09375 to 0.09375
- w_down: bfloat16 [8, 14336, 4096], P('expert', ('group', 'seq')), may hold values from -0.046875 to 0.046875
Outputs:
- layer_out: bfloat16 [32, 4096], P('expert', 'seq')
Inputs may be any that keep to these rules, and one draw needn't show every extreme that they name: `block_of_slot`: each row lists every logical block once. `routes`: the two ids of a row differ; among the 4 rows of one device no expert is named more than 2 times, and in some such blocks one expert is named exactly 2 times.
All inputs are finite; a program needn't handle non-finite values.
Results may differ from a plain program's by a relative error of at most 0.013.
Values may be sent and summed in bfloat16 or wider, within the bound.
A program may use at most 64 MiB of HBM per device.

v0:
```python
import jax
import jax.numpy as jnp
from jax import lax
from jax.sharding import PartitionSpec as P

BLOCK = 16
CAPACITY = 2


masked_score = -1e30


def copy_for_each(value, axis):
    length = lax.axis_size(axis)
    return lax.all_to_all(
        jnp.broadcast_to(value[None], (length, *value.shape)), axis, 0, 0, tiled=True
    )


def gathered_once(value, axis):
    leaves = jax.tree.leaves(value)
    turns = sorted(range(len(leaves)), key=lambda k: -leaves[k].size)
    width = (1, *leaves[turns[0]].shape)[-1]
    lines = [
        jnp.pad(leaves[k].reshape(-1), (0, -leaves[k].size % width)).reshape(-1, width)
        for k in turns
    ]
    both, at, found = (copy_for_each(jnp.concatenate(lines), axis), 0, {})
    for k, line in zip(turns, lines):
        piece = both[:, at : at + len(line)].reshape(len(both), -1)
        found[k] = piece[:, : leaves[k].size].reshape(-1, *leaves[k].shape)
        at += len(line)
    numbers = iter(range(len(leaves)))
    return jax.tree.map(lambda _: found[next(numbers)], value)


def folded_in_pairs(pieces, combine):
    while len(jax.tree.leaves(pieces)[0]) > 1:
        pieces = jax.vmap(combine)(
            *(jax.tree.map(lambda part: part[side::2], pieces) for side in (0, 1))
        )
    return jax.tree.map(lambda part: part[0], pieces)


def merged(value, axis, combine):
    pieces = gathered_once(value, axis)
    return folded_in_pairs(pieces, combine)


def of_everyone(value, axis):
    everything = copy_for_each(value, axis)
    return jnp.sum(everything, axis=0)


def laid_out(parts, dim):
    parts = jnp.moveaxis(parts, 0, dim)
    dims = parts.shape
    return parts.reshape(*dims[:dim], dims[dim] * dims[dim + 1], *dims[dim + 2 :])


def gathered_copies(value, axis, dim):
    parts = copy_for_each(value, axis)
    return laid_out(parts, dim)


def in_blocks(value, dim, length):
    before, after = (value.shape[:dim], value.shape[dim + 1 :])
    return jnp.moveaxis(value.reshape(*before, length, -1, *after), dim, 0)


def sum_at_owner(value, axis, dim):
    parts = in_blocks(value, dim, lax.axis_size(axis))
    arrived = lax.all_to_all(parts, axis, split_axis=0, concat_axis=0, tiled=True)
    return arrived.astype(jnp.float32).sum(axis=0)


def taken_together(value, axis):
    return copy_for_each(value, axis).astype(jnp.float32).sum(axis=0)


def combine_carry(earlier, later):
    high_a, total_a, sums_a = earlier
    high_b, total_b, sums_b = later
    highest = jnp.maximum(high_a, high_b)
    scale_a = jnp.exp(high_a - highest)
    scale_b = jnp.exp(high_b - highest)
    return (
        highest,
        total_a * scale_a + total_b * scale_b,
        sums_a * scale_a[..., None] + sums_b * scale_b[..., None],
    )


def shards(
    queries,
    keys,
    values,
    block_of_slot,
    lengths,
    out_proj,
    residual,
    norm_gain,
    router,
    routes,
    w_gate,
    w_up,
    w_down,
):
    batch_rows, local_heads, head_dim = queries.shape
    span_len = keys.shape[1]
    kv_local = keys.shape[2]
    per_kv = local_heads // kv_local
    grouped = queries.reshape(batch_rows, kv_local, per_kv, head_dim)
    scores = jnp.einsum(
        "rkgd,rlkd->rkgl", grouped, keys, preferred_element_type=jnp.float32
    ) * head_dim ** (-0.5)
    offsets = jnp.arange(BLOCK, dtype=jnp.int32)
    position = (block_of_slot[:, :, None] * BLOCK + offsets[None, None, :]).reshape(
        batch_rows, span_len
    )
    visible = (position < lengths[:, None])[:, None, None, :]
    masked = jnp.where(visible, scores, masked_score)
    highest = jnp.max(masked, axis=-1)
    probs = jnp.where(visible, jnp.exp(masked - highest[..., None]), 0.0)
    totals = jnp.sum(probs, axis=-1)
    weighted = jnp.einsum(
        "rkgl,rlkd->rkgd", probs.astype(jnp.bfloat16), values, preferred_element_type=jnp.float32
    )
    local_carry = (highest, totals, weighted)
    highest, totals, weighted = merged(local_carry, "seq", combine_carry)
    attended = (
        (weighted / totals[..., None])
        .astype(jnp.bfloat16)
        .reshape(batch_rows, local_heads * head_dim)
    )
    partial_value = jnp.dot(attended, out_proj, preferred_element_type=jnp.float32)
    attention = of_everyone(partial_value, "group")
    hidden = residual.astype(jnp.float32) + attention
    full_rows = gathered_copies(hidden, "seq", 1)
    meansq = jnp.mean(full_rows * full_rows, axis=-1, keepdims=True)
    normed = (full_rows * lax.rsqrt(meansq + 1e-05) * norm_gain.astype(jnp.float32)).astype(
        jnp.bfloat16
    )
    logits = jnp.dot(normed, router, preferred_element_type=jnp.float32)
    experts = router.shape[1]
    onehot = (routes[:, :, None] == jnp.arange(experts, dtype=jnp.int32)[None, None, :]).astype(
        jnp.int32
    )
    chosen = jnp.sum(onehot.astype(jnp.float32) * logits[:, None, :], axis=-1)
    gate_probs = jax.nn.softmax(chosen, axis=-1)
    per_row = jnp.sum(onehot, axis=1)
    earlier = jnp.cumsum(per_row, axis=0) - per_row
    slot_index = jnp.sum(onehot * earlier[:, None, :], axis=2)
    in_slot = (
        slot_index[:, :, None] == jnp.arange(CAPACITY, dtype=jnp.int32)[None, None, :]
    ).astype(jnp.int32)
    chart = onehot[:, :, :, None] * in_slot[:, :, None, :]
    picker = jnp.sum(chart, axis=1).astype(jnp.bfloat16)
    outbound = jnp.einsum("rec,rd->ecd", picker, normed, preferred_element_type=jnp.float32).astype(
        jnp.bfloat16
    )
    expert_devs = lax.axis_size("expert")
    local_experts = experts // expert_devs
    model_width = normed.shape[1]
    outbound = outbound.reshape(expert_devs, local_experts, CAPACITY, model_width)
    inbound = lax.all_to_all(outbound, "expert", split_axis=0, concat_axis=0, tiled=True)
    gate_act = jnp.einsum("secd,edf->secf", inbound, w_gate, preferred_element_type=jnp.float32)
    upper = jnp.einsum("secd,edf->secf", inbound, w_up, preferred_element_type=jnp.float32)
    activated = (jax.nn.silu(gate_act) * upper).astype(jnp.bfloat16)
    down_terms = jnp.einsum("secf,efd->secd", activated, w_down, preferred_element_type=jnp.float32)
    scattered = sum_at_owner(down_terms.astype(jnp.bfloat16), "seq", 3)
    my_cols = taken_together(scattered.astype(jnp.bfloat16), "group").astype(jnp.float32)
    returned = lax.all_to_all(
        my_cols.astype(jnp.bfloat16), "expert", split_axis=0, concat_axis=0, tiled=True
    )
    returned = returned.reshape(experts, CAPACITY, returned.shape[3]).astype(jnp.float32)
    mixing = jnp.sum(gate_probs[:, :, None, None] * chart.astype(jnp.float32), axis=1)
    expert_mix = jnp.einsum("rec,ecd->rd", mixing, returned)
    return (hidden + expert_mix).astype(jnp.bfloat16)


def solution(mesh):
    return jax.shard_map(
        shards,
        mesh=mesh,
        in_specs=(
            P("expert", "group", None),
            P("expert", "seq", "group", None),
            P("expert", "seq", "group", None),
            P("expert", "seq"),
            P("expert"),
            P("group", "seq"),
            P("expert", "seq"),
            P(),
            P(),
            P("expert", None),
            P("expert", None, ("group", "seq")),
            P("expert", None, ("group", "seq")),
            P("expert", ("group", "seq"), None),
        ),
        out_specs=P("expert", "seq"),
        check_vma=False,
    )
```

profile of v0, /device:TPU:1, one launch (start us, length us, event | category | flops | bytes accessed | tf_op | source)
XLA Modules:
  0.0 110.5 jit_solution(1299136599329910330)
XLA Ops:
  0.0 0.8 broadcast_multiply_fusion
  1.0 0.7 add_compare_fusion
  1.8 1.3 %fusion.69 = (f32[4,2,4]{2,1,0:T(2,128)S(1)}, f32[4,2,4,128]{3,2,1,0:T(4,128)S(1)}) fusion(bf16[4,2,4,128]{3,2,1,0:T(4,128)(2,1)} %bitcast.146, bf16[4,128,2,128]{3,2,1,0:T(2,128)(2,1)} %param.14, pred[4,128]{1,0:T(4,128)(4,1)S(1)} %add_compare_fusion), kind=kOutput, calls=%fused_computation.91 | convolution fusion | flops 1060832 | bytes 287360 | tf_op jit(solution)/shard_map/rkgd,rlkd->rkgl/dot_general | solution.py:114
  3.1 0.2 fusion.50
  3.4 1.2 %fusion.26 = f32[4,2,4,128]{3,2,1,0:T(4,128)S(1)} fusion(bf16[4,128,2,128]{3,2,1,0:T(2,128)(2,1)} %param.15, f32[4,2,4,128]{3,2,1,0:T(4,128)S(1)} %get-tuple-element.19, f32[4,2,4]{2,1,0:T(2,128)S(1)} %get-tuple-element.18, pred[4,128]{1,0:T(4,128)(4,1)S(1)} %add_compare_fusion), kind=kOutput, calls=%fused_computation.18 | convolution fusion | flops 1060864 | bytes 295552 | tf_op jit(solution)/shard_map/rkgl,rlkd->rkgd/dot_general | solution.py:126
  4.6 0.7 broadcast_in_dim.29
  5.3 11.6 %all-to-all-start = ((f32[8,34,128]{2,1,0:T(8,128)}), f32[8,34,128]{2,1,0:T(8,128)S(1)}, u32[]{:S(2)}, u32[]{:S(2)}) async-start(f32[8,34,128]{2,1,0:T(8,128)} %broadcast_in_dim.29), calls=%async_computation | async-start | bytes 327680 | tf_op jit(solution)/shard_map/all_to_all | solution.py:15
  16.9 0.8 fusion.60
  17.7 0.9 select_reduce_fusion
  18.6 0.8 fusion.59
  19.4 7.1 %all-to-all-done = f32[8,34,128]{2,1,0:T(8,128)S(1)} async-done(((f32[8,34,128]{2,1,0:T(8,128)}), f32[8,34,128]{2,1,0:T(8,128)S(1)}, u32[]{:S(2)}, u32[]{:S(2)}) %all-to-all-start) | async-done | bytes 139296 | tf_op jit(solution)/shard_map/all_to_all | solution.py:15
  26.6 0.4 slice.93
  26.9 0.4 slice.92
  27.4 0.4 slice.79
  27.8 0.4 slice.80
  28.2 0.4 slice.95
  28.6 0.4 slice.94
  28.9 0.4 slice.83
  29.3 0.4 slice.84
  29.6 0.1 copy.52
  29.8 0.1 copy.51
  29.9 0.1 copy.54
  30.2 0.2 fusion.45
  30.9 0.2 fusion.55
  31.1 0.6 broadcast_in_dim.30
  31.7 4.0 %all-to-all-start.1 = ((f32[4,4,512]{2,1,0:T(4,128)}), f32[4,4,512]{2,1,0:T(4,128)S(1)}, u32[]{:S(2)}, u32[]{:S(2)}) async-start(f32[4,4,512]{2,1,0:T(4,128)} %broadcast_in_dim.30), calls=%async_computation.1 | async-start | bytes 65536 | tf_op jit(solution)/shard_map/all_to_all | solution.py:15
  35.8 4.3 %all-to-all-done.1 = f32[4,4,512]{2,1,0:T(4,128)S(1)} async-done(((f32[4,4,512]{2,1,0:T(4,128)}), f32[4,4,512]{2,1,0:T(4,128)S(1)}, u32[]{:S(2)}, u32[]{:S(2)}) %all-to-all-start.1) | async-done | bytes 32800 | tf_op jit(solution)/shard_map/all_to_all | solution.py:15
  40.1 0.6 broadcast_in_dim.31
  40.7 3.3 %all-to-all-start.2 = ((f32[8,4,512]{2,1,0:T(4,128)}), f32[8,4,512]{2,1,0:T(4,128)S(1)}, u32[]{:S(2)}, u32[]{:S(2)}) async-start(f32[8,4,512]{2,1,0:T(4,128)} %broadcast_in_dim.31), calls=%async_computation.2 | async-start | bytes 131072 | tf_op jit(solution)/shard_map/all_to_all | solution.py:15
  44.2 9.0 %all-to-all-done.2 = f32[8,4,512]{2,1,0:T(4,128)S(1)} async-done(((f32[8,4,512]{2,1,0:T(4,128)}), f32[8,4,512]{2,1,0:T(4,128)S(1)}, u32[]{:S(2)}, u32[]{:S(2)}) %all-to-all-start.2) | async-done | bytes 65568 | tf_op jit(solution)/shard_map/all_to_all | solution.py:15
  53.1 0.1 fusion.35
  53.4 0.2 fusion
  53.6 0.1 copy.56
  53.7 14.0 %all_to_all.35 = bf16[8,1,2,4096]{3,2,1,0:T(2,128)(2,1)S(1)} all-to-all(bf16[8,1,2,4096]{3,2,1,0:T(2,128)(2,1)S(1)} %copy.56), channel_id=1, replica_groups=mesh['group'=4,'seq'=8,'expert'=8] {'expert'}, dimensions={0} | all-to-all | bytes 262144 | tf_op jit(solution)/shard_map/all_to_all | solution.py:166
  67.8 3.1 %fusion.6 = f32[8,1,2,448]{3,0,2,1:T(8,128)S(1)} fusion(bf16[1,4096,448]{1,2,0:T(8,128)(2,1)} %param.23, bf16[8,1,2,4096]{3,2,1,0:T(2,128)(2,1)S(1)} %all_to_all.35), kind=kOutput, calls=%fused_computation.8 | convolution fusion | flops 58720256 | bytes 3829760 | tf_op jit(solution)/shard_map/secd,edf->secf/dot_general | solution.py:167
  70.9 5.1 %convolution_convert_fusion = bf16[8,2,4096]{2,0,1:T(8,128)(2,1)S(1)} fusion(bf16[1,448,4096]{2,1,0:T(8,128)(2,1)} %param.25, bf16[1,4096,448]{1,2,0:T(8,128)(2,1)} %param.24, bf16[8,1,2,4096]{3,2,1,0:T(2,128)(2,1)S(1)} %all_to_all.35, f32[8,1,2,448]{3,0,2,1:T(8,128)S(1)} %fusion.6), kind=kOutput, calls=%fused_computation | convolution fusion | flops 117549056 | bytes 7630848 | tf_op jit(solution)/shard_map/secf,efd->secd/dot_general | solution.py:170
  76.0 0.7 copy.85
  76.6 3.4 %all-to-all-start.4 = ((bf16[8,8,1,2,512]{4,1,3,2,0:T(8,128)(2,1)}), bf16[8,8,1,2,512]{4,1,3,2,0:T(8,128)(2,1)S(1)}, u32[]{:S(2)}, u32[]{:S(2)}) async-start(bf16[8,8,1,2,512]{4,1,3,2,0:T(8,128)(2,1)} %bitcast.100), calls=%async_computation.4 | async-start | bytes 262144 | tf_op jit(solution)/shard_map/all_to_all | solution.py:73
  80.0 0.1 fusion.70
  80.2 0.2 multiply_reduce_fusion.1
  80.4 9.1 %all-to-all-done.4 = bf16[8,8,1,2,512]{4,1,3,2,0:T(8,128)(2,1)S(1)} async-done(((bf16[8,8,1,2,512]{4,1,3,2,0:T(8,128)(2,1)}), bf16[8,8,1,2,512]{4,1,3,2,0:T(8,128)(2,1)S(1)}, u32[]{:S(2)}, u32[]{:S(2)}) %all-to-all-start.4) | async-done | bytes 131104 | tf_op jit(solution)/shard_map/all_to_all | solution.py:73
  89.5 0.6 broadcast_in_dim.32
  90.1 3.3 %all-to-all-start.5 = ((bf16[4,8,1,2,512]{4,1,3,2,0:T(8,128)(2,1)}), bf16[4,8,1,2,512]{4,1,3,2,0:T(8,128)(2,1)S(1)}, u32[]{:S(2)}, u32[]{:S(2)}) async-start(bf16[4,8,1,2,512]{4,1,3,2,0:T(8,128)(2,1)} %broadcast_in_dim.32), calls=%async_computation.5 | async-start | bytes 131072 | tf_op jit(solution)/shard_map/all_to_all | solution.py:15
  93.4 4.4 %all-to-all-done.5 = bf16[4,8,1,2,512]{4,1,3,2,0:T(8,128)(2,1)S(1)} async-done(((bf16[4,8,1,2,512]{4,1,3,2,0:T(8,128)(2,1)}), bf16[4,8,1,2,512]{4,1,3,2,0:T(8,128)(2,1)S(1)}, u32[]{:S(2)}, u32[]{:S(2)}) %all-to-all-start.5) | async-done | bytes 65568 | tf_op jit(solution)/shard_map/all_to_all | solution.py:15
  97.8 0.6 copy.60
  98.4 6.3 %all-to-all-start.6 = ((bf16[8,1,2,512]{3,2,1,0:T(2,128)(2,1)}), bf16[8,1,2,512]{3,2,1,0:T(2,128)(2,1)S(1)}, u32[]{:S(2)}, u32[]{:S(2)}) async-start(bf16[8,1,2,512]{3,2,1,0:T(2,128)(2,1)} %copy.60), calls=%async_computation.6 | async-start | bytes 32768 | tf_op jit(solution)/shard_map/all_to_all | solution.py:173
  104.9 4.9 %all-to-all-done.6 = bf16[8,1,2,512]{3,2,1,0:T(2,128)(2,1)S(1)} async-done(((bf16[8,1,2,512]{3,2,1,0:T(2,128)(2,1)}), bf16[8,1,2,512]{3,2,1,0:T(2,128)(2,1)S(1)}, u32[]{:S(2)}, u32[]{:S(2)}) %all-to-all-start.6) | async-done | bytes 16416 | tf_op jit(solution)/shard_map/all_to_all | solution.py:173
  109.7 0.8 fusion.23
  (48 shorter events, 1.7 us)
Async XLA Ops:
  0.0 30.9 %copy-start = (bf16[1024,512]{1,0:T(8,128)(2,1)S(1)}, bf16[1024,512]{1,0:T(8,128)(2,1)}, u32[]{:S(2)}) copy-start(bf16[1024,512]{1,0:T(8,128)(2,1)} %param.18) | copy-start | bytes 3145732
  0.0 35.7 %copy-start.2 = (bf16[4096]{0:T(1024)(128)(2,1)S(1)}, bf16[4096]{0:T(1024)(128)(2,1)}, u32[]{:S(2)}) copy-start(bf16[4096]{0:T(1024)(128)(2,1)} %param.20) | copy-start | bytes 24580
  0.0 40.1 %copy-start.3 = (bf16[4,512]{1,0:T(4,128)(2,1)S(1)}, bf16[4,512]{1,0:T(4,128)(2,1)}, u32[]{:S(2)}) copy-start(bf16[4,512]{1,0:T(4,128)(2,1)} %param.19) | copy-start | bytes 12292
  5.3 21.1 %all-to-all-start = ((f32[8,34,128]{2,1,0:T(8,128)}), f32[8,34,128]{2,1,0:T(8,128)S(1)}, u32[]{:S(2)}, u32[]{:S(2)}) async-start(f32[8,34,128]{2,1,0:T(8,128)} %broadcast_in_dim.29), calls=%async_computation | async-start | bytes 327680 | tf_op jit(solution)/shard_map/all_to_all | solution.py:15
  31.7 8.3 %all-to-all-start.1 = ((f32[4,4,512]{2,1,0:T(4,128)}), f32[4,4,512]{2,1,0:T(4,128)S(1)}, u32[]{:S(2)}, u32[]{:S(2)}) async-start(f32[4,4,512]{2,1,0:T(4,128)} %broadcast_in_dim.30), calls=%async_computation.1 | async-start | bytes 65536 | tf_op jit(solution)/shard_map/all_to_all | solution.py:15
  40.7 12.4 %all-to-all-start.2 = ((f32[8,4,512]{2,1,0:T(4,128)}), f32[8,4,512]{2,1,0:T(4,128)S(1)}, u32[]{:S(2)}, u32[]{:S(2)}) async-start(f32[8,4,512]{2,1,0:T(4,128)} %broadcast_in_dim.31), calls=%async_computation.2 | async-start | bytes 131072 | tf_op jit(solution)/shard_map/all_to_all | solution.py:15
  70.9 9.1 %copy-start.4 = (bf16[4096,8]{0,1:T(8,128)(2,1)S(1)}, bf16[4096,8]{0,1:T(8,128)(2,1)}, u32[]{:S(2)}) copy-start(bf16[4096,8]{0,1:T(8,128)(2,1)} %param.21) | copy-start | bytes 196612
  70.9 9.3 %copy-start.1 = (s32[4,2]{0,1:T(2,128)S(1)}, s32[4,2]{0,1:T(2,128)}, u32[]{:S(2)}) copy-start(s32[4,2]{0,1:T(2,128)} %param.22) | copy-start | bytes 100
  76.6 12.8 %all-to-all-start.4 = ((bf16[8,8,1,2,512]{4,1,3,2,0:T(8,128)(2,1)}), bf16[8,8,1,2,512]{4,1,3,2,0:T(8,128)(2,1)S(1)}, u32[]{:S(2)}, u32[]{:S(2)}) async-start(bf16[8,8,1,2,512]{4,1,3,2,0:T(8,128)(2,1)} %bitcast.100), calls=%async_computation.4 | async-start | bytes 262144 | tf_op jit(solution)/shard_map/all_to_all | solution.py:73
  90.1 7.7 %all-to-all-start.5 = ((bf16[4,8,1,2,512]{4,1,3,2,0:T(8,128)(2,1)}), bf16[4,8,1,2,512]{4,1,3,2,0:T(8,128)(2,1)S(1)}, u32[]{:S(2)}, u32[]{:S(2)}) async-start(bf16[4,8,1,2,512]{4,1,3,2,0:T(8,128)(2,1)} %broadcast_in_dim.32), calls=%async_computation.5 | async-start | bytes 131072 | tf_op jit(solution)/shard_map/all_to_all | solution.py:15
  98.4 11.3 %all-to-all-start.6 = ((bf16[8,1,2,512]{3,2,1,0:T(2,128)(2,1)}), bf16[8,1,2,512]{3,2,1,0:T(2,128)(2,1)S(1)}, u32[]{:S(2)}, u32[]{:S(2)}) async-start(bf16[8,1,2,512]{3,2,1,0:T(2,128)(2,1)} %copy.60), calls=%async_computation.6 | async-start | bytes 32768 | tf_op jit(solution)/shard_map/all_to_all | solution.py:173
where the time goes:
time: 111 us
  waiting for transfers between devices  38.7 us (35%)
  starting transfers between devices  32 us (29%)
  blocking collectives  14 us (13%)
  matrix products  12 us (11%)
  local copies, waits for them, and re-layouts  8.19 us (7%)
  other arithmetic  5.4 us (5%)
    all_to_all x4, waiting for transfers between devices, copy_for_each(): lax.all_to_all(jnp.broadcast_to(value[None], (length, *value.shape)), axi...  24.7 us
    all_to_all x4, starting transfers between devices, copy_for_each(): lax.all_to_all(jnp.broadcast_to(value[None], (length, *value.shape)), axi...  22.3 us
    all_to_all x1, blocking collectives, shards(): lax.all_to_all(outbound, 'expert', split_axis=0, concat_axis=0, tiled=True)  14 us
    all_to_all x1, waiting for transfers between devices, sum_at_owner(): lax.all_to_all(parts, axis, split_axis=0, concat_axis=0, tiled=True)  9.06 us
    all_to_all x1, starting transfers between devices, shards(): lax.all_to_all(my_cols.astype(jnp.bfloat16), 'expert', split_axis=0, conc...  6.35 us
    dot_general x1, matrix products, shards(): jnp.einsum('secf,efd->secd', activated, w_down, preferred_element_type=jn...  5.07 us
    all_to_all x1, waiting for transfers between devices, shards(): lax.all_to_all(my_cols.astype(jnp.bfloat16), 'expert', split_axis=0, conc...  4.87 us
    all_to_all x1, starting transfers between devices, sum_at_owner(): lax.all_to_all(parts, axis, split_axis=0, concat_axis=0, tiled=True)  3.37 us
  transfers between devices with their start and end apart: 6, of which 6 were waited for; matrix products, arithmetic and copies ran while one was open for 3% of the time, Pallas kernels for 0%

commit v1 on v0

v1 whole, which is shorter than its diff:
```python
import jax
import jax.numpy as jnp
from jax import lax
from jax.experimental import pallas as pl
from jax.experimental.pallas import tpu as pltpu
from jax.sharding import PartitionSpec as P

BLOCK = 16
MASKED = -1e30
F32 = jnp.float32
BF16 = jnp.bfloat16
I32 = jnp.int32
NT = (((1,), (1,)), ((), ()))
NN = (((1,), (0,)), ((), ()))


def dot(a, b, dims=NN):
    return lax.dot_general(a, b, dims, preferred_element_type=F32)


def iota(shape, dim):
    return lax.broadcasted_iota(I32, shape, dim)


def kernel(
    blk_s, len_s, rt_s,
    q_h, k_h, v_h, wo_h, res_h, gain_h, rtr_h, wg_h, wu_h, wd_h,
    out_ref,
    q_v, k_v, v_v, wo_v, res_v, gain_v, rtr_v, wg_v, wu_v, wd_v,
    rt_buf, o1, s1, o2, s2, att, r16, b_buf, c_buf, d_buf, u_buf, gate_acc, up_acc,
    e_src, e_buf, g_src, g_buf, f16,
    local_sem, rt_send, rt_recv, a1_send, a1_recv, a2_send, a2_recv, b_send, b_recv,
    c_send, c_recv, d_send, d_recv, e_send, e_recv, g_send, g_recv,
):
    g = lax.axis_index("group")
    s = lax.axis_index("seq")
    e = lax.axis_index("expert")
    zh, y = s // 4, s % 4
    zl, core = e // 2, e % 2
    zc = zh * 8 + e
    xy = g * 4 + y

    def at(gg, ss, ee):
        return {"group": gg, "seq": ss, "expert": ee}

    def remote(src, dst, ssem, rsem, where):
        return pltpu.make_async_remote_copy(
            src_ref=src, dst_ref=dst, send_sem=ssem, recv_sem=rsem,
            device_id=where, device_id_type=pl.DeviceIdType.MESH,
        )

    pairs = [
        (q_h, q_v), (k_h, k_v), (v_h, v_v), (wo_h, wo_v), (res_h, res_v),
        (gain_h, gain_v), (rtr_h, rtr_v), (wg_h, wg_v), (wu_h, wu_v), (wd_h, wd_v),
    ]
    loads = [pltpu.make_async_copy(a, b, local_sem.at[i]) for i, (a, b) in enumerate(pairs)]
    for load in loads:
        load.start()

    barrier = pltpu.get_barrier_semaphore()

    def greet(where):
        pl.semaphore_signal(barrier, inc=1, device_id=where, device_id_type=pl.DeviceIdType.MESH)

    for d in range(1, 16):
        t = (xy + d) % 16
        greet(at(t // 4, zh * 4 + t % 4, e))
    for d in range(1, 16):
        t = (zc + d) % 16
        greet(at(g, (t // 8) * 4 + y, t % 8))
    for t in range(16):
        @pl.when(jnp.logical_not((g == zl) & (zc == t)))
        def _(t=t):
            greet(at(zl, (t // 8) * 4 + y, t % 8))

    row8, lane8 = iota((8, 128), 0), iota((8, 128), 1)
    codes = jnp.full((8, 128), -1, I32)
    count = jnp.zeros((8, 128), I32)
    for tok in range(4):
        first, second = rt_s[0, tok], rt_s[1, tok]
        hit0, hit1 = row8 == first, row8 == second
        hit = hit0 | hit1
        other = jnp.where(hit0, second, first)
        codes = jnp.where((lane8 % 4 == tok) & hit, count + 2 * other, codes)
        count = count + jnp.where(hit, 1, 0)
    rt_buf[e] = codes

    eye = iota((32, 128), 0) == iota((32, 128), 1)
    lane = iota((1, 256), 1)
    parity = iota((8, 256), 1) % 2 == iota((8, 256), 0) // 4
    for i in range(3):
        loads[i].wait()
    outs, maxes, sums = [], [], []
    for r in range(4):
        sc = dot(q_v[r], k_v[r], NT) * (128 ** -0.5)
        limit = jnp.zeros((1, 256), I32)
        for j in range(8):
            limit = jnp.where(lane // 32 == j, len_s[r] - BLOCK * blk_s[r, j], limit)
        live = parity & ((lane // 2) % BLOCK < limit)
        sc = jnp.where(live, sc, MASKED)
        m = jnp.max(sc, axis=1, keepdims=True)
        p = jnp.where(live, jnp.exp(sc - m), 0.0)
        sums.append(jnp.sum(p, axis=1, keepdims=True))
        maxes.append(m)
        outs.append(dot(p.astype(BF16), v_v[r]))

    def to_row(col):
        return jnp.sum(jnp.where(eye, col, 0.0), axis=0, keepdims=True)

    def to_col(row):
        return jnp.sum(jnp.where(eye, row, 0.0), axis=1, keepdims=True)

    o1[y] = jnp.concatenate(outs, axis=0).astype(BF16)
    s1[y, 0:1, :] = to_row(jnp.concatenate(maxes, axis=0))
    s1[y, 1:2, :] = to_row(jnp.concatenate(sums, axis=0))

    self_case = (g == zl).astype(I32)
    pl.semaphore_wait(barrier, 46 - self_case)

    sends = []
    for d in (2, 1, 3):
        to = at(g, zh * 4 + (y + d) % 4, e)
        a = remote(o1.at[y], o1.at[y], a1_send.at[2 * d], a1_recv.at[2 * y], to)
        b = remote(s1.at[y], s1.at[y], a1_send.at[2 * d + 1], a1_recv.at[2 * y + 1], to)
        a.start()
        b.start()
        sends += [a, b]
    for d in range(1, 8):
        to = at(g, s, (e + d) % 8)
        a = remote(rt_buf.at[e], rt_buf.at[e], rt_send.at[d], rt_recv.at[e], to)
        a.start()
        sends.append(a)

    me = at(g, s, e)

    def arrived(dst, rsem, ssem):
        remote(dst, dst, ssem, rsem, me).wait_recv()

    loads[4].wait()
    for j in range(4):
        r16[4 * j : 4 * j + 4, :] = res_v[:, 128 * j : 128 * (j + 1)].astype(F32)
    clane = iota((16, 256), 1)
    crow = iota((16, 256), 0)
    comb = jnp.zeros((16, 256), F32)
    clane_e, clane_blk, clane_rank = (clane // 16) % 8, (clane // 4) % 4, clane % 2
    fits = ((clane // 2) % 2 == core) & (clane_blk == crow // 4)
    ccount = jnp.zeros((16, 256), I32)
    for tok in range(4):
        hit = (clane_e == rt_s[0, tok]) | (clane_e == rt_s[1, tok])
        comb = jnp.where(fits & hit & (crow % 4 == tok) & (ccount == clane_rank), 1.0, comb)
        ccount = ccount + jnp.where(hit, 1, 0)
    comb = comb.astype(BF16)

    for d in (1, 3, 2):
        src = (y + d) % 4
        arrived(o1.at[src], a1_recv.at[2 * src], a1_send.at[0])
        arrived(s1.at[src], a1_recv.at[2 * src + 1], a1_send.at[0])
    ms = [s1[i, 0:1, :] for i in range(4)]
    top = jnp.maximum(jnp.maximum(ms[0], ms[1]), jnp.maximum(ms[2], ms[3]))
    total = jnp.zeros((1, 128), F32)
    merged = jnp.zeros((32, 128), F32)
    for i in range(4):
        w = jnp.exp(ms[i] - top)
        total = total + w * s1[i, 1:2, :]
        merged = merged + to_col(w) * o1[i].astype(F32)
    o2[zh] = merged.astype(BF16)
    s2[zh, 0:1, :] = top
    s2[zh, 1:2, :] = total
    to = at(g, (1 - zh) * 4 + y, e)
    a = remote(o2.at[zh], o2.at[zh], a2_send.at[0], a2_recv.at[0], to)
    b = remote(s2.at[zh], s2.at[zh], a2_send.at[1], a2_recv.at[1], to)
    a.start()
    b.start()
    sends += [a, b]

    for d in range(1, 8):
        src = (e + d) % 8
        arrived(rt_buf.at[src], rt_recv.at[src], rt_send.at[0])
    lane1 = iota((1, 128), 1)
    code = jnp.full((1, 128), -1, I32)
    for i in range(8):
        mine = jnp.sum(jnp.where(row8 == e, rt_buf[i], 0), axis=0, keepdims=True)
        code = jnp.where(lane1 // 16 == i, mine, code)
    rank = jnp.where(code >= 0, code % 2, -1)
    other_lane = jnp.where(code >= 0, code // 2, 0)
    srow, slane = iota((64, 128), 0), iota((64, 128), 1)
    pick = (
        (srow % 2 == rank) & ((srow // 2) % 8 == slane // 16) & (srow // 16 == (slane // 4) % 4)
    )
    select = jnp.where(pick, 1.0, 0.0).astype(BF16)
    other_col = jnp.sum(
        jnp.where(pick[0:16], other_lane.astype(F32), 0.0), axis=1, keepdims=True
    )
    eye16 = iota((16, 128), 0) == iota((16, 128), 1)

    def to_row16(col):
        return jnp.sum(jnp.where(eye16, col, 0.0), axis=0, keepdims=True)[:, 0:16]

    other_row = to_row16(other_col)
    loads[3].wait()

    arrived(o2.at[1 - zh], a2_recv.at[0], a2_send.at[0])
    arrived(s2.at[1 - zh], a2_recv.at[1], a2_send.at[1])
    top = jnp.maximum(s2[0, 0:1, :], s2[1, 0:1, :])
    w0, w1 = jnp.exp(s2[0, 0:1, :] - top), jnp.exp(s2[1, 0:1, :] - top)
    total = w0 * s2[0, 1:2, :] + w1 * s2[1, 1:2, :]
    merged = to_col(w0 / total) * o2[0].astype(F32) + to_col(w1 / total) * o2[1].astype(F32)
    att[0:32, :] = merged
    att[32:64, :] = merged
    part = jnp.zeros((8, 512), F32)
    for h in range(8):
        part = part + dot(att[pl.ds(h, 8, stride=8), :].astype(BF16), wo_v[128 * h : 128 * (h + 1), :])
    low = iota((8, 128), 0) < 4
    for j in range(2):
        b_buf[g, 8 * j : 8 * j + 8, :] = jnp.where(
            low, part[:, 256 * j : 256 * j + 128], part[:, 256 * j + 128 : 256 * j + 256]
        )
    for d in (2, 1, 3):
        a = remote(b_buf.at[g], b_buf.at[g], b_send.at[d], b_recv.at[g], at((g + d) % 4, s, e))
        a.start()
        sends.append(a)
    for d in (1, 3, 2):
        src = (g + d) % 4
        arrived(b_buf.at[src], b_recv.at[src], b_send.at[0])
    hidden = ((b_buf[0] + b_buf[1]) + (b_buf[2] + b_buf[3])) + r16[...]
    c_buf[zc] = hidden.astype(BF16)
    for d in (8, 7, 9, 6, 10, 5, 11, 4, 12, 3, 13, 2, 14, 1, 15):
        t = (zc + d) % 16
        a = remote(
            c_buf.at[zc], c_buf.at[zc], c_send.at[d], c_recv.at[zc],
            at(g, (t // 8) * 4 + y, t % 8),
        )
        a.start()
        sends.append(a)
    for i in range(5, 9):
        loads[i].wait()

    for half in range(2):
        zz = (zh + half) % 2
        for d in range(half == 0, 8):
            src = zz * 8 + (e + d) % 8
            arrived(c_buf.at[src], c_recv.at[src], c_send.at[0])
        rows = c_buf[pl.ds(zz * 8, 8)].reshape(128, 128)
        taken = dot(select, rows).astype(BF16)
        for j in range(4):
            d_buf[y, zz, :, 128 * j : 128 * (j + 1)] = taken[16 * j : 16 * j + 16]
        for d in (2, 1, 3):
            a = remote(
                d_buf.at[y, zz], d_buf.at[y, zz], d_send.at[2 * d + half], d_recv.at[2 * y + zz],
                at(g, zh * 4 + (y + d) % 4, e),
            )
            a.start()
            sends.append(a)

    square = jnp.zeros((16, 1), F32)
    logits = jnp.zeros((8, 16), F32)
    for n, d in enumerate((0, 1, 3, 2)):
        src = (y + d) % 4
        for half in range(2):
            zz = (zh + half) % 2
            if d:
                arrived(d_buf.at[src, zz], d_recv.at[2 * src + zz], d_send.at[0])
            x = d_buf[src, zz].astype(F32)
            square = square + jnp.sum(x * x, axis=1, keepdims=True)
            cols = pl.ds(pl.multiple_of((zz * 4 + src) * 512, 512), 512)
            u = (x * gain_v[0:1, cols].astype(F32)).astype(BF16)
            logits = logits + dot(rtr_v[:, cols], u, NT)
            gg, uu = dot(wg_v[:, cols], u, NT), dot(wu_v[:, cols], u, NT)
            if n == 0 and half == 0:
                gate_acc[...] = gg
                up_acc[...] = uu
            else:
                gate_acc[...] += gg
                up_acc[...] += uu
    scale = to_row16(lax.rsqrt(square * (1.0 / 4096.0) + 1e-05))
    logits = logits * scale
    lrow = iota((8, 16), 0)
    own = jnp.sum(jnp.where(lrow == e, logits, 0.0), axis=0, keepdims=True)
    oth = jnp.sum(jnp.where(lrow.astype(F32) == other_row, logits, 0.0), axis=0, keepdims=True)
    share = 1.0 / (1.0 + jnp.exp(oth - own))
    gate = gate_acc[...] * scale
    act = gate / (1.0 + jnp.exp(-gate)) * (up_acc[...] * (scale * share))
    act = act.T.astype(BF16)
    loads[9].wait()

    for dy in (2, 1, 3, 0):
        ty = (y + dy) % 4
        for zz in range(2):
            cols = pl.ds(pl.multiple_of((zz * 4 + ty) * 512, 512), 512)
            res = dot(act, wd_v[:, cols])
            for tx in range(4):
                tiles = []
                for j in range(2):
                    first = res[8 * (tx // 2) : 8 * (tx // 2) + 8, 256 * j : 256 * j + 128]
                    second = res[8 * (tx // 2) : 8 * (tx // 2) + 8, 256 * j + 128 : 256 * j + 256]
                    if tx % 2:
                        first = pltpu.roll(first, 4, 0)
                    else:
                        second = pltpu.roll(second, 4, 0)
                    tiles.append(jnp.where(low, first, second))
                e_src[tx * 4 + ty, 16 * zz : 16 * zz + 16, :] = jnp.concatenate(tiles, axis=0).astype(BF16)
        for dx in (2, 1, 3, 0):
            if dx or dy:
                t = ((g + dx) % 4) * 4 + ty
                a = remote(
                    e_src.at[t], e_buf.at[xy], e_send.at[4 * dx + dy], e_recv.at[xy],
                    at((g + dx) % 4, zh * 4 + ty, e),
                )
                a.start()
                sends.append(a)
    summed = e_src[xy].astype(F32)
    for dy in (0, 1, 3, 2):
        for dx in (0, 1, 3, 2):
            if dx or dy:
                src = ((g + dx) % 4) * 4 + (y + dy) % 4
                arrived(e_buf.at[src], e_recv.at[src], e_send.at[0])
                summed = summed + e_buf[src].astype(F32)
    for zz in range(2):
        g_src[zz] = summed[16 * zz : 16 * zz + 16].astype(BF16)
    later = []
    for zz in range(2):
        for tx in range(4):
            for cc in range(2):
                ee = g * 2 + cc
                same = (g == tx) & (zh == zz) & (e == ee)
                a = remote(
                    g_src.at[zz], g_buf.at[zc], g_send.at[zz * 8 + tx * 2 + cc], g_recv.at[zc],
                    at(tx, zz * 4 + y, ee),
                )
                pl.when(jnp.logical_not(same))(a.start)
                later.append((same, a))

    @pl.when(g == zl)
    def _():
        g_buf[zc] = g_src[zh]

    for t in range(16):
        @pl.when(jnp.logical_not((g == zl) & (zc == t)))
        def _(t=t):
            arrived(g_buf.at[t], g_recv.at[t], g_send.at[0])
    final = hidden + dot(comb, g_buf[...].reshape(256, 128))
    f16[...] = final
    for j in range(4):
        out_ref[:, 128 * j : 128 * (j + 1)] = f16[4 * j : 4 * j + 4, :].astype(BF16)

    for a in sends:
        a.wait_send()
    for same, a in later:
        pl.when(jnp.logical_not(same))(a.wait_send)


def shards(
    queries, keys, values, block_of_slot, lengths, out_proj, residual, norm_gain, router,
    routes, w_gate, w_up, w_down,
):
    args = (
        block_of_slot, lengths, routes.T,
        queries, keys.reshape(4, 256, 128), values.reshape(4, 256, 128), out_proj, residual,
        norm_gain.reshape(1, 4096), router.T, w_gate[0].T, w_up[0].T, w_down[0],
    )
    smem = pl.BlockSpec(memory_space=pltpu.SMEM)
    hbm = pl.BlockSpec(memory_space=pltpu.HBM)
    dma = pltpu.SemaphoreType.DMA
    vmem = pltpu.VMEM
    return pl.pallas_call(
        kernel,
        out_shape=jax.ShapeDtypeStruct((4, 512), BF16),
        in_specs=[smem] * 3 + [hbm] * 10,
        out_specs=pl.BlockSpec(memory_space=pltpu.VMEM),
        scratch_shapes=[vmem(a.shape, a.dtype) for a in args[3:]]
        + [
            vmem((8, 8, 128), I32),
            vmem((4, 32, 128), BF16), vmem((4, 2, 128), F32),
            vmem((2, 32, 128), BF16), vmem((2, 2, 128), F32),
            vmem((64, 128), F32), vmem((16, 128), F32), vmem((4, 16, 128), F32),
            vmem((16, 16, 128), BF16), vmem((4, 2, 16, 512), BF16), vmem((16, 512), BF16),
            vmem((448, 16), F32), vmem((448, 16), F32),
            vmem((16, 32, 128), BF16), vmem((16, 32, 128), BF16),
            vmem((2, 16, 128), BF16), vmem((16, 16, 128), BF16), vmem((16, 128), F32),
            dma((10,)), dma((8,)), dma((8,)), dma((8,)), dma((8,)), dma((2,)), dma((2,)),
            dma((4,)), dma((4,)), dma((16,)), dma((16,)), dma((8,)), dma((8,)),
            dma((16,)), dma((16,)), dma((16,)), dma((16,)),
        ],
        compiler_params=pltpu.CompilerParams(
            collective_id=0, has_side_effects=True, vmem_limit_bytes=67043328
        ),
    )(*args)


def solution(mesh):
    return jax.shard_map(
        shards,
        mesh=mesh,
        in_specs=(
            P("expert", "group", None),
            P("expert", "seq", "group", None),
            P("expert", "seq", "group", None),
            P("expert", "seq"),
            P("expert"),
            P("group", "seq"),
            P("expert", "seq"),
            P(),
            P(),
            P("expert", None),
            P("expert", None, ("group", "seq")),
            P("expert", None, ("group", "seq")),
            P("expert", ("group", "seq"), None),
        ),
        out_specs=P("expert", "seq"),
        check_vma=False,
    )
```

time: 111 us -> 49.4 us (0.45)
  Pallas kernels: 0 us -> 46.6 us
  waiting for transfers between devices: 38.7 us -> 0 us
  starting transfers between devices: 32 us -> 0 us
  blocking collectives: 14 us -> 0 us
  matrix products: 12 us -> 0 us
  local copies, waits for them, and re-layouts: 8.19 us -> 2.57 us
  other arithmetic: 5.4 us -> 0 us
    pallas_call x0 -> x1, Pallas kernels: none -> 46.6 us  [shards(): pl.pallas_call(kernel, out_shape=jax.ShapeDtypeStruct((4, 512), BF16), in...]
    all_to_all x6 -> x0, waiting for transfers between devices: 38.7 us -> none  [the longest x4 24.7 us: copy_for_each(): lax.all_to_all(jnp.broadcast_to(value[None], (length, *value.shape)), axi...]
    all_to_all x6 -> x0, starting transfers between devices: 32 us -> none  [the longest x4 22.3 us: copy_for_each(): lax.all_to_all(jnp.broadcast_to(value[None], (length, *value.shape)), axi...]
    all_to_all x1 -> x0, blocking collectives: 14 us -> none  [shards(): lax.all_to_all(outbound, 'expert', split_axis=0, concat_axis=0, tiled=True)]
    dot_general x8 -> x0, matrix products: 12 us -> none  [the longest x1 5.07 us: shards(): jnp.einsum('secf,efd->secd', activated, w_down, preferred_element_type=jn...]
    slice x12 -> x0, local copies, waits for them, and re-layouts: 2.94 us -> none  [the longest x8 2.91 us: folded_in_pairs(): part[side::2]]
    broadcast_in_dim x4 -> x0, local copies, waits for them, and re-layouts: 2.54 us -> none  [copy_for_each(): jnp.broadcast_to(value[None], (length, *value.shape))]
    reduce_sum x11 -> x0, other arithmetic: 2.37 us -> none  [the longest x1 0.89 us: shards(): slot_index = jnp.sum(onehot * earlier[:, None, :], axis=2)]
  transfers between devices with their start and end apart: 6 -> 0, of which waited for: 6 -> 0; matrix products, arithmetic and copies ran while one was open for 3% -> 0% of each run, Pallas kernels for 0% -> 0%
where the time goes in v1:
time: 49.4 us; the launch traced here: 49.2 us
  Pallas kernels  46.6 us (94%)
  local copies, waits for them, and re-layouts  2.57 us (5%)
    pallas_call x1, Pallas kernels, shards(): pl.pallas_call(kernel, out_shape=jax.ShapeDtypeStruct((4, 512), BF16), in...  46.6 us
    reshape x1, local copies, waits for them, and re-layouts, shards(): norm_gain.reshape(1, 4096)  1.3 us
    unnamed x1, local copies, waits for them, and re-layouts  1.27 us

profile of v1, /device:TPU:1, one launch (start us, length us, event | category | flops | bytes accessed | tf_op | source)
XLA Modules:
  0.0 49.2 jit_solution(12800338842503448426)
XLA Ops:
  0.0 1.3 %reshape.11.gain_h = bf16[1,4096]{1,0:T(2,128)(2,1)} reshape(bf16[4096]{0:T(1024)(128)(2,1)} %param.20) | data formatting | bytes 16384 | tf_op jit(solution)/shard_map/reshape | solution.py:359
  1.3 46.6 %shard_map.127 = bf16[4,512]{1,0:T(4,128)(2,1)} custom-call(s32[4,8]{1,0:T(4,128)} %blk_s.1, s32[4]{0:T(128)} %len_s.1, s32[2,4]{1,0:T(2,128)} %bitcast.17, bf16[4,8,128]{2,1,0:T(8,128)(2,1)} %q_h.1, bf16[4,256,128]{2,1,0:T(8,128)(2,1)} %bitcast.14, bf16[4,256,128]{2,1,0:T(8,128)(2,1)} %bitcast.15, bf16[1024,512]{1,0:T(8,128)(2,1)} %wo_h.1, ...), custom_call_target="tpu_custom_call" | custom-call | tf_op jit(solution)/shard_map/pallas_call | solution.py:365
  48.0 1.3 %copy.15 = bf16[4,512]{1,0:T(4,128)(2,1)} copy(bf16[4,512]{1,0:T(4,128)(2,1)} %shard_map.127) | data formatting | bytes 8192

commit v2 on v1

--- a/solution.py
+++ b/solution.py
@@ -23,22 +23,29 @@
 
 
 def kernel(
-    blk_s, len_s, rt_s,
+    blk_h, len_h, rt_h,
     q_h, k_h, v_h, wo_h, res_h, gain_h, rtr_h, wg_h, wu_h, wd_h,
     out_ref,
+    blk_s, len_s, rt_s,
     q_v, k_v, v_v, wo_v, res_v, gain_v, rtr_v, wg_v, wu_v, wd_v,
-    rt_buf, o1, s1, o2, s2, att, r16, b_buf, c_buf, d_buf, u_buf, gate_acc, up_acc,
+    rt_buf, o1, s1, gain_f, att, r16, b_buf, c_buf, d_buf, u_buf, gate_acc, up_acc,
     e_src, e_buf, g_src, g_buf, f16,
-    local_sem, rt_send, rt_recv, a1_send, a1_recv, a2_send, a2_recv, b_send, b_recv,
+    local_sem, rt_send, rt_recv, a1_send, a1_recv, small_sem, b_send, b_recv,
     c_send, c_recv, d_send, d_recv, e_send, e_recv, g_send, g_recv,
 ):
     g = lax.axis_index("group")
     s = lax.axis_index("seq")
     e = lax.axis_index("expert")
-    zh, y = s // 4, s % 4
-    zl, core = e // 2, e % 2
+    zh, y = lax.div(s, 4), lax.rem(s, 4)
+    zl, core = lax.div(e, 2), lax.rem(e, 2)
     zc = zh * 8 + e
     xy = g * 4 + y
+    oz = 1 - zh
+    gs = [g] + [lax.rem(g + d, 4) for d in (1, 2, 3)]
+    ys = [y] + [lax.rem(y + d, 4) for d in (1, 2, 3)]
+    es = [e] + [lax.rem(e + d, 8) for d in range(1, 8)]
+    zs = [zh, oz]
+    peers = [zs[d // 4] * 4 + ys[d % 4] for d in range(8)]
 
     def at(gg, ss, ee):
         return {"group": gg, "seq": ss, "expert": ee}
@@ -49,30 +56,33 @@
             device_id=where, device_id_type=pl.DeviceIdType.MESH,
         )
 
+    barrier = pltpu.get_barrier_semaphore()
+
+    def greet(where):
+        pl.semaphore_signal(barrier, inc=1, device_id=where, device_id_type=pl.DeviceIdType.MESH)
+
+    for d in (6, 5, 7, 4, 2, 1, 3):
+        greet(at(g, peers[d], e))
+    for dz in (1, 0):
+        for de in (4, 3, 5, 2, 6, 1, 7):
+            greet(at(g, peers[4 * dz], es[de]))
+    for d in (2, 1, 3):
+        greet(at(gs[d], s, e))
+
     pairs = [
         (q_h, q_v), (k_h, k_v), (v_h, v_v), (wo_h, wo_v), (res_h, res_v),
         (gain_h, gain_v), (rtr_h, rtr_v), (wg_h, wg_v), (wu_h, wu_v), (wd_h, wd_v),
     ]
     loads = [pltpu.make_async_copy(a, b, local_sem.at[i]) for i, (a, b) in enumerate(pairs)]
-    for load in loads:
+    small = [
+        pltpu.make_async_copy(a, b, small_sem.at[i])
+        for i, (a, b) in enumerate([(rt_h, rt_s), (blk_h, blk_s), (len_h, len_s)])
+    ]
+    for load in loads[0:3] + small:
         load.start()
 
-    barrier = pltpu.get_barrier_semaphore()
-
-    def greet(where):
-        pl.semaphore_signal(barrier, inc=1, device_id=where, device_id_type=pl.DeviceIdType.MESH)
-
-    for d in range(1, 16):
-        t = (xy + d) % 16
-        greet(at(t // 4, zh * 4 + t % 4, e))
-    for d in range(1, 16):
-        t = (zc + d) % 16
-        greet(at(g, (t // 8) * 4 + y, t % 8))
-    for t in range(16):
-        @pl.when(jnp.logical_not((g == zl) & (zc == t)))
-        def _(t=t):
-            greet(at(zl, (t // 8) * 4 + y, t % 8))
-
+    for copy in small:
+        copy.wait()
     row8, lane8 = iota((8, 128), 0), iota((8, 128), 1)
     codes = jnp.full((8, 128), -1, I32)
     count = jnp.zeros((8, 128), I32)
@@ -90,6 +100,8 @@
     parity = iota((8, 256), 1) % 2 == iota((8, 256), 0) // 4
     for i in range(3):
         loads[i].wait()
+    for load in loads[3:]:
+        load.start()
     outs, maxes, sums = [], [], []
     for r in range(4):
         sc = dot(q_v[r], k_v[r], NT) * (128 ** -0.5)
@@ -110,23 +122,22 @@
     def to_col(row):
         return jnp.sum(jnp.where(eye, row, 0.0), axis=1, keepdims=True)
 
-    o1[y] = jnp.concatenate(outs, axis=0).astype(BF16)
-    s1[y, 0:1, :] = to_row(jnp.concatenate(maxes, axis=0))
-    s1[y, 1:2, :] = to_row(jnp.concatenate(sums, axis=0))
-
-    self_case = (g == zl).astype(I32)
-    pl.semaphore_wait(barrier, 46 - self_case)
+    o1[s] = jnp.concatenate(outs, axis=0).astype(BF16)
+    s1[s, 0:1, :] = to_row(jnp.concatenate(maxes, axis=0))
+    s1[s, 1:2, :] = to_row(jnp.concatenate(sums, axis=0))
+
+    pl.semaphore_wait(barrier, 24)
 
     sends = []
-    for d in (2, 1, 3):
-        to = at(g, zh * 4 + (y + d) % 4, e)
-        a = remote(o1.at[y], o1.at[y], a1_send.at[2 * d], a1_recv.at[2 * y], to)
-        b = remote(s1.at[y], s1.at[y], a1_send.at[2 * d + 1], a1_recv.at[2 * y + 1], to)
+    for d in (6, 5, 7, 4, 2, 1, 3):
+        to = at(g, peers[d], e)
+        a = remote(o1.at[s], o1.at[s], a1_send.at[2 * d], a1_recv.at[2 * s], to)
+        b = remote(s1.at[s], s1.at[s], a1_send.at[2 * d + 1], a1_recv.at[2 * s + 1], to)
         a.start()
         b.start()
         sends += [a, b]
     for d in range(1, 8):
-        to = at(g, s, (e + d) % 8)
+        to = at(g, s, es[d])
         a = remote(rt_buf.at[e], rt_buf.at[e], rt_send.at[d], rt_recv.at[e], to)
         a.start()
         sends.append(a)
@@ -151,30 +162,8 @@
         ccount = ccount + jnp.where(hit, 1, 0)
     comb = comb.astype(BF16)
 
-    for d in (1, 3, 2):
-        src = (y + d) % 4
-        arrived(o1.at[src], a1_recv.at[2 * src], a1_send.at[0])
-        arrived(s1.at[src], a1_recv.at[2 * src + 1], a1_send.at[0])
-    ms = [s1[i, 0:1, :] for i in range(4)]
-    top = jnp.maximum(jnp.maximum(ms[0], ms[1]), jnp.maximum(ms[2], ms[3]))
-    total = jnp.zeros((1, 128), F32)
-    merged = jnp.zeros((32, 128), F32)
-    for i in range(4):
-        w = jnp.exp(ms[i] - top)
-        total = total + w * s1[i, 1:2, :]
-        merged = merged + to_col(w) * o1[i].astype(F32)
-    o2[zh] = merged.astype(BF16)
-    s2[zh, 0:1, :] = top
-    s2[zh, 1:2, :] = total
-    to = at(g, (1 - zh) * 4 + y, e)
-    a = remote(o2.at[zh], o2.at[zh], a2_send.at[0], a2_recv.at[0], to)
-    b = remote(s2.at[zh], s2.at[zh], a2_send.at[1], a2_recv.at[1], to)
-    a.start()
-    b.start()
-    sends += [a, b]
-
     for d in range(1, 8):
-        src = (e + d) % 8
+        src = es[d]
         arrived(rt_buf.at[src], rt_recv.at[src], rt_send.at[0])
     lane1 = iota((1, 128), 1)
     code = jnp.full((1, 128), -1, I32)
@@ -197,14 +186,25 @@
         return jnp.sum(jnp.where(eye16, col, 0.0), axis=0, keepdims=True)[:, 0:16]
 
     other_row = to_row16(other_col)
+    loads[5].wait()
+    gain_f[...] = gain_v[...].astype(F32)
     loads[3].wait()
 
-    arrived(o2.at[1 - zh], a2_recv.at[0], a2_send.at[0])
-    arrived(s2.at[1 - zh], a2_recv.at[1], a2_send.at[1])
-    top = jnp.maximum(s2[0, 0:1, :], s2[1, 0:1, :])
-    w0, w1 = jnp.exp(s2[0, 0:1, :] - top), jnp.exp(s2[1, 0:1, :] - top)
-    total = w0 * s2[0, 1:2, :] + w1 * s2[1, 1:2, :]
-    merged = to_col(w0 / total) * o2[0].astype(F32) + to_col(w1 / total) * o2[1].astype(F32)
+    for d in (1, 3, 2, 4, 5, 7, 6):
+        src = peers[d]
+        arrived(o1.at[src], a1_recv.at[2 * src], a1_send.at[0])
+        arrived(s1.at[src], a1_recv.at[2 * src + 1], a1_send.at[0])
+    ms = [s1[i, 0:1, :] for i in range(8)]
+    top = ms[0]
+    for m in ms[1:]:
+        top = jnp.maximum(top, m)
+    ws = [jnp.exp(m - top) for m in ms]
+    total = jnp.zeros((1, 128), F32)
+    for i in range(8):
+        total = total + ws[i] * s1[i, 1:2, :]
+    merged = jnp.zeros((32, 128), F32)
+    for i in range(8):
+        merged = merged + to_col(ws[i] / total) * o1[i].astype(F32)
     att[0:32, :] = merged
     att[32:64, :] = merged
     part = jnp.zeros((8, 512), F32)
@@ -216,29 +216,30 @@
             low, part[:, 256 * j : 256 * j + 128], part[:, 256 * j + 128 : 256 * j + 256]
         )
     for d in (2, 1, 3):
-        a = remote(b_buf.at[g], b_buf.at[g], b_send.at[d], b_recv.at[g], at((g + d) % 4, s, e))
+        a = remote(b_buf.at[g], b_buf.at[g], b_send.at[d], b_recv.at[g], at(gs[d], s, e))
         a.start()
         sends.append(a)
     for d in (1, 3, 2):
-        src = (g + d) % 4
+        src = gs[d]
         arrived(b_buf.at[src], b_recv.at[src], b_send.at[0])
     hidden = ((b_buf[0] + b_buf[1]) + (b_buf[2] + b_buf[3])) + r16[...]
     c_buf[zc] = hidden.astype(BF16)
-    for d in (8, 7, 9, 6, 10, 5, 11, 4, 12, 3, 13, 2, 14, 1, 15):
-        t = (zc + d) % 16
-        a = remote(
-            c_buf.at[zc], c_buf.at[zc], c_send.at[d], c_recv.at[zc],
-            at(g, (t // 8) * 4 + y, t % 8),
-        )
-        a.start()
-        sends.append(a)
-    for i in range(5, 9):
+    for de in (4, 3, 5, 2, 6, 1, 7, 0):
+        for dz in (1, 0):
+            if de or dz:
+                a = remote(
+                    c_buf.at[zc], c_buf.at[zc], c_send.at[8 * dz + de], c_recv.at[zc],
+                    at(g, peers[4 * dz], es[de]),
+                )
+                a.start()
+                sends.append(a)
+    for i in range(6, 9):
         loads[i].wait()
 
     for half in range(2):
-        zz = (zh + half) % 2
+        zz = zs[half]
         for d in range(half == 0, 8):
-            src = zz * 8 + (e + d) % 8
+            src = zz * 8 + es[d]
             arrived(c_buf.at[src], c_recv.at[src], c_send.at[0])
         rows = c_buf[pl.ds(zz * 8, 8)].reshape(128, 128)
         taken = dot(select, rows).astype(BF16)
@@ -247,7 +248,7 @@
         for d in (2, 1, 3):
             a = remote(
                 d_buf.at[y, zz], d_buf.at[y, zz], d_send.at[2 * d + half], d_recv.at[2 * y + zz],
-                at(g, zh * 4 + (y + d) % 4, e),
+                at(g, peers[d], e),
             )
             a.start()
             sends.append(a)
@@ -255,36 +256,41 @@
     square = jnp.zeros((16, 1), F32)
     logits = jnp.zeros((8, 16), F32)
     for n, d in enumerate((0, 1, 3, 2)):
-        src = (y + d) % 4
+        src = ys[d]
+        gg, uu = jnp.zeros((448, 16), F32), jnp.zeros((448, 16), F32)
         for half in range(2):
-            zz = (zh + half) % 2
+            zz = zs[half]
             if d:
                 arrived(d_buf.at[src, zz], d_recv.at[2 * src + zz], d_send.at[0])
             x = d_buf[src, zz].astype(F32)
             square = square + jnp.sum(x * x, axis=1, keepdims=True)
-            cols = pl.ds(pl.multiple_of((zz * 4 + src) * 512, 512), 512)
-            u = (x * gain_v[0:1, cols].astype(F32)).astype(BF16)
+            block = zz * 4 + src
+            cols = pl.ds(pl.multiple_of(block * 512, 512), 512)
+            scales = gain_f[pl.ds(pl.multiple_of(block * 4, 4), 4), :]
+            u = jnp.concatenate(
+                [(x[:, 128 * j : 128 * (j + 1)] * scales[j : j + 1]).astype(BF16) for j in range(4)], axis=1
+            )
             logits = logits + dot(rtr_v[:, cols], u, NT)
-            gg, uu = dot(wg_v[:, cols], u, NT), dot(wu_v[:, cols], u, NT)
-            if n == 0 and half == 0:
-                gate_acc[...] = gg
-                up_acc[...] = uu
-            else:
-                gate_acc[...] += gg
-                up_acc[...] += uu
+            gg, uu = gg + dot(wg_v[:, cols], u, NT), uu + dot(wu_v[:, cols], u, NT)
+        if n == 0:
+            gate_acc[...] = gg
+            up_acc[...] = uu
+        elif n < 3:
+            gate_acc[...] += gg
+            up_acc[...] += uu
     scale = to_row16(lax.rsqrt(square * (1.0 / 4096.0) + 1e-05))
     logits = logits * scale
     lrow = iota((8, 16), 0)
     own = jnp.sum(jnp.where(lrow == e, logits, 0.0), axis=0, keepdims=True)
     oth = jnp.sum(jnp.where(lrow.astype(F32) == other_row, logits, 0.0), axis=0, keepdims=True)
     share = 1.0 / (1.0 + jnp.exp(oth - own))
-    gate = gate_acc[...] * scale
-    act = gate / (1.0 + jnp.exp(-gate)) * (up_acc[...] * (scale * share))
+    gate = (gate_acc[...] + gg) * scale
+    act = gate / (1.0 + jnp.exp(-gate)) * ((up_acc[...] + uu) * (scale * share))
     act = act.T.astype(BF16)
     loads[9].wait()
 
     for dy in (2, 1, 3, 0):
-        ty = (y + dy) % 4
+        ty = ys[dy]
         for zz in range(2):
             cols = pl.ds(pl.multiple_of((zz * 4 + ty) * 512, 512), 512)
             res = dot(act, wd_v[:, cols])
@@ -301,10 +307,10 @@
                 e_src[tx * 4 + ty, 16 * zz : 16 * zz + 16, :] = jnp.concatenate(tiles, axis=0).astype(BF16)
         for dx in (2, 1, 3, 0):
             if dx or dy:
-                t = ((g + dx) % 4) * 4 + ty
+                t = gs[dx] * 4 + ty
                 a = remote(
                     e_src.at[t], e_buf.at[xy], e_send.at[4 * dx + dy], e_recv.at[xy],
-                    at((g + dx) % 4, zh * 4 + ty, e),
+                    at(gs[dx], peers[dy], e),
                 )
                 a.start()
                 sends.append(a)
@@ -312,7 +318,7 @@
     for dy in (0, 1, 3, 2):
         for dx in (0, 1, 3, 2):
             if dx or dy:
-                src = ((g + dx) % 4) * 4 + (y + dy) % 4
+                src = gs[dx] * 4 + ys[dy]
                 arrived(e_buf.at[src], e_recv.at[src], e_send.at[0])
                 summed = summed + e_buf[src].astype(F32)
     for zz in range(2):
@@ -356,28 +362,27 @@
     args = (
         block_of_slot, lengths, routes.T,
         queries, keys.reshape(4, 256, 128), values.reshape(4, 256, 128), out_proj, residual,
-        norm_gain.reshape(1, 4096), router.T, w_gate[0].T, w_up[0].T, w_down[0],
+        norm_gain.reshape(32, 128), router.T, w_gate[0].T, w_up[0].T, w_down[0],
     )
-    smem = pl.BlockSpec(memory_space=pltpu.SMEM)
     hbm = pl.BlockSpec(memory_space=pltpu.HBM)
     dma = pltpu.SemaphoreType.DMA
     vmem = pltpu.VMEM
     return pl.pallas_call(
         kernel,
         out_shape=jax.ShapeDtypeStruct((4, 512), BF16),
-        in_specs=[smem] * 3 + [hbm] * 10,
+        in_specs=[hbm] * 13,
         out_specs=pl.BlockSpec(memory_space=pltpu.VMEM),
-        scratch_shapes=[vmem(a.shape, a.dtype) for a in args[3:]]
+        scratch_shapes=[pltpu.SMEM(a.shape, a.dtype) for a in args[:3]]
+        + [vmem(a.shape, a.dtype) for a in args[3:]]
         + [
             vmem((8, 8, 128), I32),
-            vmem((4, 32, 128), BF16), vmem((4, 2, 128), F32),
-            vmem((2, 32, 128), BF16), vmem((2, 2, 128), F32),
+            vmem((8, 32, 128), BF16), vmem((8, 2, 128), F32), vmem((32, 128), F32),
             vmem((64, 128), F32), vmem((16, 128), F32), vmem((4, 16, 128), F32),
             vmem((16, 16, 128), BF16), vmem((4, 2, 16, 512), BF16), vmem((16, 512), BF16),
             vmem((448, 16), F32), vmem((448, 16), F32),
             vmem((16, 32, 128), BF16), vmem((16, 32, 128), BF16),
             vmem((2, 16, 128), BF16), vmem((16, 16, 128), BF16), vmem((16, 128), F32),
-            dma((10,)), dma((8,)), dma((8,)), dma((8,)), dma((8,)), dma((2,)), dma((2,)),
+            dma((10,)), dma((8,)), dma((8,)), dma((16,)), dma((16,)), dma((3,)),
             dma((4,)), dma((4,)), dma((16,)), dma((16,)), dma((8,)), dma((8,)),
             dma((16,)), dma((16,)), dma((16,)), dma((16,)),
         ],

time: 49.4 us -> 44.4 us (0.90)
  Pallas kernels: 46.6 us -> 43 us
  local copies, waits for them, and re-layouts: 2.57 us -> 1.28 us
    pallas_call x1, Pallas kernels: 46.6 us -> 43 us  [shards(): pl.pallas_call(kernel, out_shape=jax.ShapeDtypeStruct((4, 512), BF16), in...]
    reshape x1 -> x0, local copies, waits for them, and re-layouts: 1.3 us -> none  [shards(): norm_gain.reshape(1, 4096)]
where the time goes in v2:
time: 44.4 us; the launch traced here: 44.3 us
  Pallas kernels  43 us (97%)
  local copies, waits for them, and re-layouts  1.28 us (3%)
    pallas_call x1, Pallas kernels, shards(): pl.pallas_call(kernel, out_shape=jax.ShapeDtypeStruct((4, 512), BF16), in...  43 us
    unnamed x1, local copies, waits for them, and re-layouts  1.28 us

profile of v2, /device:TPU:1, one launch (start us, length us, event | category | flops | bytes accessed | tf_op | source)
XLA Modules:
  0.0 44.3 jit_solution(5304155001191795745)
XLA Ops:
  0.0 43.0 %shard_map.127 = bf16[4,512]{1,0:T(4,128)(2,1)} custom-call(s32[4,8]{1,0:T(4,128)} %blk_h.1, s32[4]{0:T(128)} %len_h.1, s32[2,4]{1,0:T(2,128)} %bitcast.19, bf16[4,8,128]{2,1,0:T(8,128)(2,1)} %q_h.1, bf16[4,256,128]{2,1,0:T(8,128)(2,1)} %bitcast.15, bf16[4,256,128]{2,1,0:T(8,128)(2,1)} %bitcast.16, bf16[1024,512]{1,0:T(8,128)(2,1)} %wo_h.1, ...), custom_call_target="tpu_custom_call" | custom-call | tf_op jit(solution)/shard_map/pallas_call | solution.py:370
  43.0 1.3 %copy.15 = bf16[4,512]{1,0:T(4,128)(2,1)} copy(bf16[4,512]{1,0:T(4,128)(2,1)} %shard_map.127) | data formatting | bytes 8192

commit v3 on v2

--- a/solution.py
+++ b/solution.py
@@ -28,7 +28,7 @@
     out_ref,
     blk_s, len_s, rt_s,
     q_v, k_v, v_v, wo_v, res_v, gain_v, rtr_v, wg_v, wu_v, wd_v,
-    rt_buf, o1, s1, gain_f, att, r16, b_buf, c_buf, d_buf, u_buf, gate_acc, up_acc,
+    rt_buf, o1, s1, gain_f, att, r16, b_buf, c_src, c_buf, d_buf, wgt, wut, gate_acc, up_acc,
     e_src, e_buf, g_src, g_buf, f16,
     local_sem, rt_send, rt_recv, a1_send, a1_recv, small_sem, b_send, b_recv,
     c_send, c_recv, d_send, d_recv, e_send, e_recv, g_send, g_recv,
@@ -161,6 +161,20 @@
         comb = jnp.where(fits & hit & (crow % 4 == tok) & (ccount == clane_rank), 1.0, comb)
         ccount = ccount + jnp.where(hit, 1, 0)
     comb = comb.astype(BF16)
+    prow, pcol = iota((64, 16), 0), iota((64, 16), 1)
+    pfits = (prow // 2) % 4 == pcol // 4
+    pack = jnp.zeros((64, 16), F32)
+    pcount = jnp.zeros((64, 16), I32)
+    for tok in range(4):
+        hit = (prow // 8 == rt_s[0, tok]) | (prow // 8 == rt_s[1, tok])
+        pack = jnp.where(pfits & hit & (pcol % 4 == tok) & (pcount == prow % 2), 1.0, pack)
+        pcount = pcount + jnp.where(hit, 1, 0)
+    pack = pack.astype(BF16)
+    urow, ucol = iota((64, 64), 0), iota((64, 64), 1)
+    unpack = jnp.where(
+        (urow % 2 == ucol % 2) & ((urow // 2) % 8 == ucol // 8) & (urow // 16 == (ucol // 2) % 4),
+        1.0, 0.0,
+    ).astype(BF16)
 
     for d in range(1, 8):
         src = es[d]
@@ -172,13 +186,10 @@
         code = jnp.where(lane1 // 16 == i, mine, code)
     rank = jnp.where(code >= 0, code % 2, -1)
     other_lane = jnp.where(code >= 0, code // 2, 0)
-    srow, slane = iota((64, 128), 0), iota((64, 128), 1)
-    pick = (
-        (srow % 2 == rank) & ((srow // 2) % 8 == slane // 16) & (srow // 16 == (slane // 4) % 4)
-    )
-    select = jnp.where(pick, 1.0, 0.0).astype(BF16)
+    srow, slane = iota((16, 128), 0), iota((16, 128), 1)
+    pick = (srow % 2 == rank) & (srow // 2 == slane // 16) & ((slane // 4) % 4 == 0)
     other_col = jnp.sum(
-        jnp.where(pick[0:16], other_lane.astype(F32), 0.0), axis=1, keepdims=True
+        jnp.where(pick, other_lane.astype(F32), 0.0), axis=1, keepdims=True
     )
     eye16 = iota((16, 128), 0) == iota((16, 128), 1)
 
@@ -186,6 +197,15 @@
         return jnp.sum(jnp.where(eye16, col, 0.0), axis=0, keepdims=True)[:, 0:16]
 
     other_row = to_row16(other_col)
+    def turn(first, last):
+        for n in range(first, last):
+            src, dst = ((wg_v, wgt), (wu_v, wut))[n // 8]
+            rows = pl.ds(512 * (n % 8), 512)
+            dst[rows, :] = src[:, rows].T
+
+    for i in (7, 8):
+        loads[i].wait()
+    turn(0, 9)
     loads[5].wait()
     gain_f[...] = gain_v[...].astype(F32)
     loads[3].wait()
@@ -223,26 +243,29 @@
         src = gs[d]
         arrived(b_buf.at[src], b_recv.at[src], b_send.at[0])
     hidden = ((b_buf[0] + b_buf[1]) + (b_buf[2] + b_buf[3])) + r16[...]
-    c_buf[zc] = hidden.astype(BF16)
+    packed = dot(pack, hidden.astype(BF16)).astype(BF16)
+    for i in range(8):
+        c_src[i] = packed[8 * i : 8 * i + 8]
+    c_buf[zc] = c_src[e]
     for de in (4, 3, 5, 2, 6, 1, 7, 0):
         for dz in (1, 0):
             if de or dz:
                 a = remote(
-                    c_buf.at[zc], c_buf.at[zc], c_send.at[8 * dz + de], c_recv.at[zc],
+                    c_src.at[es[de]], c_buf.at[zc], c_send.at[8 * dz + de], c_recv.at[zc],
                     at(g, peers[4 * dz], es[de]),
                 )
                 a.start()
                 sends.append(a)
-    for i in range(6, 9):
-        loads[i].wait()
+    loads[6].wait()
+    turn(9, 16)
 
     for half in range(2):
         zz = zs[half]
         for d in range(half == 0, 8):
             src = zz * 8 + es[d]
             arrived(c_buf.at[src], c_recv.at[src], c_send.at[0])
-        rows = c_buf[pl.ds(zz * 8, 8)].reshape(128, 128)
-        taken = dot(select, rows).astype(BF16)
+        rows = c_buf[pl.ds(zz * 8, 8)].astype(F32).reshape(64, 128).astype(BF16)
+        taken = dot(unpack, rows).astype(BF16)
         for j in range(4):
             d_buf[y, zz, :, 128 * j : 128 * (j + 1)] = taken[16 * j : 16 * j + 16]
         for d in (2, 1, 3):
@@ -257,7 +280,7 @@
     logits = jnp.zeros((8, 16), F32)
     for n, d in enumerate((0, 1, 3, 2)):
         src = ys[d]
-        gg, uu = jnp.zeros((448, 16), F32), jnp.zeros((448, 16), F32)
+        gg, uu = jnp.zeros((16, 448), F32), jnp.zeros((16, 448), F32)
         for half in range(2):
             zz = zs[half]
             if d:
@@ -271,7 +294,7 @@
                 [(x[:, 128 * j : 128 * (j + 1)] * scales[j : j + 1]).astype(BF16) for j in range(4)], axis=1
             )
             logits = logits + dot(rtr_v[:, cols], u, NT)
-            gg, uu = gg + dot(wg_v[:, cols], u, NT), uu + dot(wu_v[:, cols], u, NT)
+            gg, uu = gg + dot(u, wgt[cols, :]), uu + dot(u, wut[cols, :])
         if n == 0:
             gate_acc[...] = gg
             up_acc[...] = uu
@@ -279,14 +302,18 @@
             gate_acc[...] += gg
             up_acc[...] += uu
     scale = to_row16(lax.rsqrt(square * (1.0 / 4096.0) + 1e-05))
+    factor = lax.rsqrt(square * (1.0 / 4096.0) + 1e-05)
     logits = logits * scale
     lrow = iota((8, 16), 0)
     own = jnp.sum(jnp.where(lrow == e, logits, 0.0), axis=0, keepdims=True)
     oth = jnp.sum(jnp.where(lrow.astype(F32) == other_row, logits, 0.0), axis=0, keepdims=True)
     share = 1.0 / (1.0 + jnp.exp(oth - own))
-    gate = (gate_acc[...] + gg) * scale
-    act = gate / (1.0 + jnp.exp(-gate)) * ((up_acc[...] + uu) * (scale * share))
-    act = act.T.astype(BF16)
+    share_col = jnp.sum(
+        jnp.where(iota((16, 16), 0) == iota((16, 16), 1), share, 0.0), axis=1, keepdims=True
+    )
+    gate = (gate_acc[...] + gg) * factor
+    act = gate / (1.0 + jnp.exp(-gate)) * ((up_acc[...] + uu) * (factor * share_col))
+    act = act.astype(BF16)
     loads[9].wait()
 
     for dy in (2, 1, 3, 0):
@@ -378,8 +405,8 @@
             vmem((8, 8, 128), I32),
             vmem((8, 32, 128), BF16), vmem((8, 2, 128), F32), vmem((32, 128), F32),
             vmem((64, 128), F32), vmem((16, 128), F32), vmem((4, 16, 128), F32),
-            vmem((16, 16, 128), BF16), vmem((4, 2, 16, 512), BF16), vmem((16, 512), BF16),
-            vmem((448, 16), F32), vmem((448, 16), F32),
+            vmem((8, 8, 128), BF16), vmem((16, 8, 128), BF16), vmem((4, 2, 16, 512), BF16), vmem((4096, 448), BF16), vmem((4096, 448), BF16),
+            vmem((16, 448), F32), vmem((16, 448), F32),
             vmem((16, 32, 128), BF16), vmem((16, 32, 128), BF16),
             vmem((2, 16, 128), BF16), vmem((16, 16, 128), BF16), vmem((16, 128), F32),
             dma((10,)), dma((8,)), dma((8,)), dma((16,)), dma((16,)), dma((3,)),

time: 44.4 us -> 44.1 us (level)
  no operation moved by 1% of the time
where the time goes in v3:
time: 44.1 us; the launch traced here: 44 us
  Pallas kernels  42.7 us (97%)
  local copies, waits for them, and re-layouts  1.28 us (3%)
    pallas_call x1, Pallas kernels, shards(): pl.pallas_call(kernel, out_shape=jax.ShapeDtypeStruct((4, 512), BF16), in...  42.7 us
    unnamed x1, local copies, waits for them, and re-layouts  1.28 us

profile of v3, /device:TPU:1, one launch (start us, length us, event | category | flops | bytes accessed | tf_op | source)
XLA Modules:
  0.0 44.0 jit_solution(13652228449533466698)
XLA Ops:
  0.0 42.7 %shard_map.127 = bf16[4,512]{1,0:T(4,128)(2,1)} custom-call(s32[4,8]{1,0:T(4,128)} %blk_h.1, s32[4]{0:T(128)} %len_h.1, s32[2,4]{1,0:T(2,128)} %bitcast.19, bf16[4,8,128]{2,1,0:T(8,128)(2,1)} %q_h.1, bf16[4,256,128]{2,1,0:T(8,128)(2,1)} %bitcast.15, bf16[4,256,128]{2,1,0:T(8,128)(2,1)} %bitcast.16, bf16[1024,512]{1,0:T(8,128)(2,1)} %wo_h.1, ...), custom_call_target="tpu_custom_call" | custom-call | tf_op jit(solution)/shard_map/pallas_call | solution.py:397
  42.7 1.3 %copy.15 = bf16[4,512]{1,0:T(4,128)(2,1)} copy(bf16[4,512]{1,0:T(4,128)(2,1)} %shard_map.127) | data formatting | bytes 8192
